TPU v7x, 512 devices: a whole 4x8x8 slice. The times are simulated.
512 devices in a mesh: row: 8 (over y), col: 32 (over z, x), layer: 2 (over core).
Axes of the slice: x: 4, y: 8, z: 8, core: 2. Of those that a mesh axis runs over, the one named last changes fastest.
Arguments:
- anomaly_x: bfloat16 [8, 4096, 4096], P(None, 'row', ('layer', 'col')), may hold values from -0.09375 to 0.09375
- anomaly_y: bfloat16 [8, 4096, 4096], P(None, 'col', ('layer', 'row')), may hold values from -6 to 6
Outputs:
- covariance: bfloat16 [8, 4096, 4096], P('layer', 'row', 'col')
All inputs are finite; a program needn't handle non-finite values.
Results may differ from a plain program's by a relative error of at most 0.001.
Values may be sent and summed in bfloat16 or wider, within the bound.
A program may use at most 64 MiB of HBM per device.

v0:
```python
import jax
import jax.numpy as jnp
from jax import lax
from jax.sharding import PartitionSpec as P


def copy_for_each(x, axis):
    copies = jnp.broadcast_to(x, (lax.axis_size(axis), *x.shape))
    return lax.all_to_all(copies, axis, split_axis=0, concat_axis=0, tiled=True)


def laid_out(tiles, dim):
    lengths = list(tiles.shape[1:])
    lengths[dim] *= tiles.shape[0]
    return jnp.moveaxis(tiles, 0, dim).reshape(lengths)


def collect(x, axis, dim):
    tiles = copy_for_each(x, axis)
    return laid_out(tiles, dim)


def cut_along(x, dim, peers):
    before, after = (x.shape[:dim], x.shape[dim + 1 :])
    return jnp.moveaxis(x.reshape(*before, peers, -1, *after), dim, 0)


def sent_and_summed(x, axis, dim):
    peers = lax.axis_size(axis)
    tiles = lax.all_to_all(cut_along(x, dim, peers), axis, 0, 0, tiled=True)
    return jnp.sum(tiles, axis=0)


def on_device(anomaly_x, anomaly_y):
    panel_x = lax.all_gather(anomaly_x, "col", axis=2, tiled=True)
    partial_tile = jnp.einsum(
        "bik,bjk->bij", panel_x, collect(anomaly_y, "row", 2), preferred_element_type=jnp.float32
    )
    summed = sent_and_summed(partial_tile, "layer", 0)
    return summed.astype(jnp.bfloat16)


def solution(mesh):
    placed = (P(None, "row", ("layer", "col")), P(None, "col", ("layer", "row")))
    return jax.shard_map(
        on_device, mesh=mesh, in_specs=placed, out_specs=P("layer", "row", "col"), check_vma=False
    )
```

profile of v0, /device:TPU:1, one launch (start us, length us, event | category | flops | bytes accessed | tf_op | source)
XLA Modules:
  0.0 185.4 jit_solution(12335205534793210125)
XLA Ops:
  6.5 0.0 all-gather.2.cloned.1.call-start
  6.5 0.7 all-gather.2.cloned.1.call-update
  7.3 1.6 broadcast_in_dim.3
  8.8 100.8 %all_to_all.10 = bf16[8,8,128,256]{3,2,1,0:T(8,128)(2,1)S(1)} all-to-all(bf16[8,8,128,256]{3,2,1,0:T(8,128)(2,1)S(1)} %broadcast_in_dim.3), channel_id=1, replica_groups=mesh['row'=8,'col'=32,'layer'=2] {'row'}, dimensions={0} | all-to-all | bytes 8388608 | tf_op jit(solution)/shard_map/all_to_all | solution.py:9
  109.6 2.5 %copy.4 = bf16[8,8,16,8,256]{4,3,0,2,1:T(8,128)(2,1)} copy(bf16[8,8,16,8,256]{4,3,2,1,0:T(8,128)(2,1)S(1)} %bitcast.6) | data formatting | bytes 8388608 | tf_op jit(solution)/shard_map/reshape | solution.py:15
  112.1 49.1 %all-gather.2.cloned.1.call-done = bf16[8,512,2048]{1,2,0:T(8,128)(2,1)} async-done(((bf16[8,512,64]{1,2,0:T(8,128)(2,1)}), bf16[8,512,2048]{1,2,0:T(8,128)(2,1)}) %all-gather.2.cloned.1.call-update) | async-done | bytes 16777232 | tf_op jit(solution)/shard_map/all_gather | solution.py:35
  161.2 9.8 %fusion = f32[8,512,128]{2,1,0:T(8,128)S(1)} fusion(bf16[8,512,2048]{1,2,0:T(8,128)(2,1)} %all-gather.2.cloned.1.call-done, bf16[8,128,2048]{2,1,0:T(8,128)(2,1)} %bitcast.7), kind=kOutput, calls=%fused_computation | convolution fusion | flops 2147483648 | bytes 23068672 | tf_op jit(solution)/shard_map/bik,bjk->bij/dot_general | solution.py:36
  171.1 6.4 %all_to_all.11 = f32[2,4,512,128]{3,2,1,0:T(8,128)S(1)} all-to-all(f32[2,4,512,128]{3,2,1,0:T(8,128)S(1)} %bitcast.8), channel_id=1, replica_groups=mesh['row'=8,'col'=32,'layer'=2] {'layer'}, dimensions={0} | all-to-all | bytes 4194304 | tf_op jit(solution)/shard_map/all_to_all | solution.py:30
  177.5 1.1 reduce_sum.9
Async XLA Ops:
  6.5 154.7 %all-gather.2.cloned.1.call-start = ((), (), s32[]{:S(2)}) async-start(), calls=%async_computation.2 | async-start | bytes 17301504 | tf_op jit(solution)/shard_map/all_gather | solution.py:35
Sparse Core Ops, SparseCore 0:
  10.5 150.6 all-gather.1
where the time goes:
time: 186 us; the launch traced here: 185 us
  blocking collectives  107 us (58%)
  waiting for transfers between devices  49.8 us (27%)
  between operations  13.4 us (7%)
  matrix products  9.82 us (5%)
  local copies, waits for them, and re-layouts  4.08 us (2%)
    all_to_all x1, blocking collectives, copy_for_each(): return lax.all_to_all(copies, axis, split_axis=0, concat_axis=0, tiled=True)  101 us
    all_gather x1, waiting for transfers between devices, on_device(): panel_x = lax.all_gather(anomaly_x, 'col', axis=2, tiled=True)  49.1 us
    dot_general x1, matrix products, on_device(): jnp.einsum('bik,bjk->bij', panel_x, collect(anomaly_y, 'row', 2), preferr...  9.82 us
    all_to_all x1, blocking collectives, sent_and_summed(): tiles = lax.all_to_all(cut_along(x, dim, peers), axis, 0, 0, tiled=True)  6.45 us
  transfers between devices with their start and end apart: 1, of which 1 were waited for; matrix products, arithmetic and copies ran while one was open for 2% of the time, Pallas kernels for 0%

commit v1 on v0

v1 whole, which is shorter than its diff:
```python
import jax
import jax.numpy as jnp
from jax import lax
from jax.experimental import pallas as pl
from jax.experimental.pallas import tpu as pltpu
from jax.sharding import PartitionSpec as P

MESH = pl.DeviceIdType.MESH
RING = 8
LINE = 4
OFFSETS = (0, 1, 3, 2)
BACK = (0, 2, 1, 3)


def kernel(
    x_hbm, y_hbm, out_ref, x_in, y_in, xg, yg, acc, tile, in_sem, own_sem,
    a_send, a_recv, g_send, g_recv, c_send, c_recv,
):
    row, col, layer = lax.axis_index("row"), lax.axis_index("col"), lax.axis_index("layer")
    z, x = col // LINE, lax.rem(col, LINE)
    mine = layer * LINE + x

    def at(row_to, z_to, x_to, layer_to):
        return {"row": row_to, "col": z_to * LINE + x_to, "layer": layer_to}

    def step_x(p):
        return lax.rem(x + OFFSETS[p], LINE)

    def along(pos, by):
        return lax.rem(pos + by + RING, RING)

    pos = (z, row)
    inputs = (x_in, y_in)
    gathered = (xg, yg)
    depth = (64, 128)

    def place(kind, chunk, part, x_from):
        span = pl.ds(pl.multiple_of(x_from * depth[kind], depth[kind]), depth[kind])
        return gathered[kind].at[chunk, part, span, :]

    def neighbour(kind, by):
        if kind == 0:
            return at(row, along(z, by), x, layer)
        return at(along(row, by), z, x, layer)

    loads = [
        pltpu.make_async_copy(x_hbm, x_in, in_sem.at[0]),
        pltpu.make_async_copy(y_hbm, y_in, in_sem.at[1]),
    ]
    own = [
        pltpu.make_async_copy(x_hbm.at[mine], place(0, z, layer, x), own_sem.at[0]),
        pltpu.make_async_copy(y_hbm.at[mine], place(1, row, layer, x), own_sem.at[1]),
    ]
    for copy in loads + own:
        copy.start()

    barrier = pltpu.get_barrier_semaphore()
    other = 1 - layer
    peers = [at(row, z, x, other)]
    peers += [at(row, z, step_x(p), to) for p in (1, 2, 3) for to in (0, 1)]
    peers += [neighbour(kind, by) for kind in (0, 1) for by in (1, -1)]
    for peer in peers:
        pl.semaphore_signal(barrier, inc=1, device_id=peer, device_id_type=MESH)
    acc[...] = jnp.zeros_like(acc)
    pl.semaphore_wait(barrier, len(peers))
    for copy in loads:
        copy.wait()

    def deal(kind, p, to):
        x_to = step_x(p)
        return pltpu.make_async_remote_copy(
            src_ref=inputs[kind].at[to * LINE + x_to],
            dst_ref=place(kind, pos[kind], layer, x),
            send_sem=a_send.at[kind, p, to],
            recv_sem=a_recv.at[kind, BACK[p], layer],
            device_id=at(row, z, x_to, to),
            device_id_type=MESH,
        )

    def dealt(kind, p, origin):
        block = place(kind, pos[kind], origin, step_x(p))
        return pltpu.make_async_remote_copy(
            src_ref=block,
            dst_ref=block,
            send_sem=a_send.at[kind, p, origin],
            recv_sem=a_recv.at[kind, p, origin],
            device_id=at(row, z, x, other),
            device_id_type=MESH,
        )

    deals = [deal(kind, 0, other) for kind in (0, 1)]
    deals += [deal(kind, p, to) for p in (1, 2, 3) for kind in (0, 1) for to in (0, 1)]
    for copy in deals:
        copy.start()

    def piece(kind, chunk, p):
        return place(kind, chunk, slice(None), step_x(p))

    def forward(kind, way, step, p):
        by = 1 if way == 0 else -1
        chunk = along(pos[kind], -by * step)
        block = piece(kind, chunk, p)
        return pltpu.make_async_remote_copy(
            src_ref=block,
            dst_ref=block,
            send_sem=g_send.at[kind, way, step, p],
            recv_sem=g_recv.at[kind, chunk, p],
            device_id=neighbour(kind, by),
            device_id_type=MESH,
        )

    def arrived(kind, way, step, p):
        by = 1 if way == 0 else -1
        chunk = along(pos[kind], -by * step)
        block = piece(kind, chunk, p)
        return pltpu.make_async_remote_copy(
            src_ref=block,
            dst_ref=block,
            send_sem=g_send.at[kind, way, 0, p],
            recv_sem=g_recv.at[kind, chunk, p],
            device_id=neighbour(kind, by),
            device_id_type=MESH,
        )

    def apart(a, b):
        return jnp.minimum(lax.rem(a - b + RING, RING), lax.rem(b - a + RING, RING))

    def multiply(step):
        def body(chunk, carry):
            @pl.when(jnp.maximum(apart(chunk, z), apart(chunk, row)) == step)
            def _():
                total = acc[...]
                for part in (0, 1):
                    total += jnp.dot(yg[chunk, part], xg[chunk, part], preferred_element_type=jnp.float32)
                acc[...] = total

            return carry

        lax.fori_loop(0, RING, body, 0)

    forwards = []
    for step in range(5):
        for p in range(LINE):
            for kind in (0, 1):
                if step == 0:
                    if p == 0:
                        own[kind].wait()
                        dealt(kind, 0, other).wait_recv()
                    else:
                        dealt(kind, p, 0).wait_recv()
                        dealt(kind, p, 1).wait_recv()
                for way in (0, 1):
                    odd = p % 2 == way
                    if step == 4 and not odd:
                        continue
                    if step > 0:
                        arrived(kind, way, step, p).wait_recv()
                    if step < 3 or (step == 3 and odd):
                        copy = forward(kind, way, step, p)
                        copy.start()
                        forwards.append(copy)
        multiply(step)

    def hand(p):
        x_to = step_x(p)
        return pltpu.make_async_remote_copy(
            src_ref=tile.at[p],
            dst_ref=out_ref.at[x],
            send_sem=c_send.at[p],
            recv_sem=c_recv.at[BACK[p]],
            device_id=at(row, z, x_to, layer),
            device_id_type=MESH,
        )

    def handed(p):
        block = out_ref.at[step_x(p)]
        return pltpu.make_async_remote_copy(
            src_ref=block,
            dst_ref=block,
            send_sem=c_send.at[p],
            recv_sem=c_recv.at[p],
            device_id=at(row, z, step_x(p), layer),
            device_id_type=MESH,
        )

    hands = []
    for p in (3, 1, 2, 0):
        x_to = step_x(p)
        rows = acc[pl.ds(pl.multiple_of(x_to * 128, 128), 128), :]
        block = rows.T.astype(jnp.bfloat16)
        if p == 0:
            out_ref[x] = block
        else:
            tile[p] = block
            copy = hand(p)
            copy.start()
            hands.append(copy)
    for copy in deals + forwards + hands:
        copy.wait_send()
    for p in (1, 2, 3):
        handed(p).wait_recv()


def on_device(anomaly_x, anomaly_y):
    dma = pltpu.SemaphoreType.DMA
    return pl.pallas_call(
        kernel,
        out_shape=jax.ShapeDtypeStruct((4, 512, 128), jnp.bfloat16),
        in_specs=[pl.BlockSpec(memory_space=pl.ANY)] * 2,
        out_specs=pl.BlockSpec(memory_space=pltpu.VMEM),
        scratch_shapes=[
            pltpu.VMEM((8, 64, 512), jnp.bfloat16),
            pltpu.VMEM((8, 128, 256), jnp.bfloat16),
            pltpu.VMEM((RING, 2, 256, 512), jnp.bfloat16),
            pltpu.VMEM((RING, 2, 512, 256), jnp.bfloat16),
            pltpu.VMEM((512, 512), jnp.float32),
            pltpu.VMEM((LINE, 512, 128), jnp.bfloat16),
            dma((2,)),
            dma((2,)),
            dma((2, LINE, 2)),
            dma((2, LINE, 2)),
            dma((2, 2, 4, LINE)),
            dma((2, RING, LINE)),
            dma((LINE,)),
            dma((LINE,)),
        ],
        compiler_params=pltpu.CompilerParams(collective_id=0, has_side_effects=True),
    )(jnp.transpose(anomaly_x, (0, 2, 1)), anomaly_y)


def solution(mesh):
    placed = (P(None, "row", ("layer", "col")), P(None, "col", ("layer", "row")))
    return jax.shard_map(
        on_device, mesh=mesh, in_specs=placed, out_specs=P("layer", "row", "col"), check_vma=False
    )
```

time: 186 us -> 72.7 us (0.39)
  blocking collectives: 107 us -> 0 us
  Pallas kernels: 0 us -> 70.7 us
  waiting for transfers between devices: 49.8 us -> 0 us
  between operations: 13.4 us -> 0.01 us
  matrix products: 9.82 us -> 0 us
  local copies, waits for them, and re-layouts: 4.08 us -> 1.87 us
    all_to_all x2 -> x0, blocking collectives: 107 us -> none  [the longest x1 101 us: copy_for_each(): return lax.all_to_all(copies, axis, split_axis=0, concat_axis=0, tiled=True)]
    pallas_call x0 -> x1, Pallas kernels: none -> 70.7 us  [on_device(): pl.pallas_call(kernel, out_shape=jax.ShapeDtypeStruct((4, 512, 128), jnp....]
    all_gather x1 -> x0, waiting for transfers between devices: 49.1 us -> none  [on_device(): panel_x = lax.all_gather(anomaly_x, 'col', axis=2, tiled=True)]
    dot_general x1 -> x0, matrix products: 9.82 us -> none  [on_device(): jnp.einsum('bik,bjk->bij', panel_x, collect(anomaly_y, 'row', 2), preferr...]
    reshape x1 -> x0, local copies, waits for them, and re-layouts: 2.52 us -> none  [laid_out(): return jnp.moveaxis(tiles, 0, dim).reshape(lengths)]
    unnamed x0 -> x1, local copies, waits for them, and re-layouts: none -> 1.87 us
  transfers between devices with their start and end apart: 1 -> 0, of which waited for: 1 -> 0; matrix products, arithmetic and copies ran while one was open for 2% -> 0% of each run, Pallas kernels for 0% -> 0%
where the time goes in v1:
time: 72.7 us; the launch traced here: 72.6 us
  Pallas kernels  70.7 us (97%)
  local copies, waits for them, and re-layouts  1.87 us (3%)
    pallas_call x1, Pallas kernels, on_device(): pl.pallas_call(kernel, out_shape=jax.ShapeDtypeStruct((4, 512, 128), jnp....  70.7 us
    unnamed x1, local copies, waits for them, and re-layouts  1.87 us

profile of v1, /device:TPU:1, one launch (start us, length us, event | category | flops | bytes accessed | tf_op | source)
XLA Modules:
  0.0 72.6 jit_solution(11531591131459417632)
XLA Ops:
  0.0 70.7 %shard_map.28 = bf16[4,512,128]{2,1,0:T(8,128)(2,1)} custom-call(bf16[8,64,512]{2,1,0:T(8,128)(2,1)} %bitcast.1, bf16[8,128,256]{2,1,0:T(8,128)(2,1)} %y_hbm.1), custom_call_target="tpu_custom_call" | custom-call | tf_op jit(solution)/shard_map/pallas_call | solution.py:206
  70.7 1.9 %copy.4 = bf16[4,512,128]{2,1,0:T(8,128)(2,1)} copy(bf16[4,512,128]{2,1,0:T(8,128)(2,1)} %shard_map.28) | data formatting | bytes 1048576

commit v2 on v1

--- a/solution.py
+++ b/solution.py
@@ -10,11 +10,21 @@
 LINE = 4
 OFFSETS = (0, 1, 3, 2)
 BACK = (0, 2, 1, 3)
+ORDERS = (
+    (
+        ((0, 0), (0, 1), (0, 2), (1, 0), (0, 3), (2, 0), (1, 3), (1, 1), (3, 0), (2, 3), (1, 2), (2, 1), (3, 3), (2, 2)),
+        ((0, 0), (0, 1), (0, 2), (1, 1), (1, 2), (0, 3), (2, 1), (2, 2), (1, 0), (3, 1), (1, 3), (2, 0), (3, 2), (2, 3)),
+    ),
+    (
+        ((0, 0), (1, 0), (0, 1), (0, 2), (1, 1), (0, 3), (1, 2), (1, 3), (2, 2), (2, 3), (2, 0), (3, 3), (2, 1), (3, 0)),
+        ((0, 0), (1, 0), (0, 1), (0, 2), (1, 1), (0, 3), (1, 2), (1, 3), (2, 2), (2, 1), (3, 2), (2, 3), (3, 1), (2, 0)),
+    ),
+)
 
 
 def kernel(
     x_hbm, y_hbm, out_ref, x_in, y_in, xg, yg, acc, tile, in_sem, own_sem,
-    a_send, a_recv, g_send, g_recv, c_send, c_recv,
+    a_send, a_recv, g_send, g_recv, l_send, l_recv, c_send, c_recv,
 ):
     row, col, layer = lax.axis_index("row"), lax.axis_index("col"), lax.axis_index("layer")
     z, x = col // LINE, lax.rem(col, LINE)
@@ -61,7 +71,6 @@
     peers += [neighbour(kind, by) for kind in (0, 1) for by in (1, -1)]
     for peer in peers:
         pl.semaphore_signal(barrier, inc=1, device_id=peer, device_id_type=MESH)
-    acc[...] = jnp.zeros_like(acc)
     pl.semaphore_wait(barrier, len(peers))
     for copy in loads:
         copy.wait()
@@ -89,7 +98,8 @@
         )
 
     deals = [deal(kind, 0, other) for kind in (0, 1)]
-    deals += [deal(kind, p, to) for p in (1, 2, 3) for kind in (0, 1) for to in (0, 1)]
+    deals += [deal(kind, p, to) for kind in (0, 1) for p in (1, 2) for to in (0, 1)]
+    deals += [deal(kind, 3, to) for kind in (0, 1) for to in (0, 1)]
     for copy in deals:
         copy.start()
 
@@ -122,90 +132,168 @@
             device_id_type=MESH,
         )
 
-    def apart(a, b):
-        return jnp.minimum(lax.rem(a - b + RING, RING), lax.rem(b - a + RING, RING))
-
-    def multiply(step):
-        def body(chunk, carry):
-            @pl.when(jnp.maximum(apart(chunk, z), apart(chunk, row)) == step)
-            def _():
-                total = acc[...]
-                for part in (0, 1):
-                    total += jnp.dot(yg[chunk, part], xg[chunk, part], preferred_element_type=jnp.float32)
-                acc[...] = total
-
-            return carry
-
-        lax.fori_loop(0, RING, body, 0)
-
-    forwards = []
-    for step in range(5):
-        for p in range(LINE):
-            for kind in (0, 1):
-                if step == 0:
-                    if p == 0:
-                        own[kind].wait()
-                        dealt(kind, 0, other).wait_recv()
-                    else:
-                        dealt(kind, p, 0).wait_recv()
-                        dealt(kind, p, 1).wait_recv()
-                for way in (0, 1):
-                    odd = p % 2 == way
-                    if step == 4 and not odd:
-                        continue
-                    if step > 0:
-                        arrived(kind, way, step, p).wait_recv()
-                    if step < 3 or (step == 3 and odd):
-                        copy = forward(kind, way, step, p)
-                        copy.start()
-                        forwards.append(copy)
-        multiply(step)
-
-    def hand(p):
-        x_to = step_x(p)
-        return pltpu.make_async_remote_copy(
-            src_ref=tile.at[p],
-            dst_ref=out_ref.at[x],
-            send_sem=c_send.at[p],
-            recv_sem=c_recv.at[BACK[p]],
-            device_id=at(row, z, x_to, layer),
-            device_id_type=MESH,
-        )
-
-    def handed(p):
-        block = out_ref.at[step_x(p)]
-        return pltpu.make_async_remote_copy(
-            src_ref=block,
-            dst_ref=block,
-            send_sem=c_send.at[p],
-            recv_sem=c_recv.at[p],
+    def quarter(q):
+        return pl.ds(q * 128, 128)
+
+    def last(way, step, p, q):
+        by = 1 if way == 0 else -1
+        block = piece(0, along(z, -by * step), p).at[:, :, quarter(q)]
+        sem = (way, step - 2, q)
+        return pltpu.make_async_remote_copy(
+            src_ref=block,
+            dst_ref=block,
+            send_sem=l_send.at[sem],
+            recv_sem=l_recv.at[sem],
+            device_id=neighbour(0, by),
+            device_id_type=MESH,
+        )
+
+    def last_arrived(way, step, p, q):
+        by = 1 if way == 0 else -1
+        block = piece(0, along(z, -by * (step + 1)), p).at[:, :, quarter(q)]
+        sem = (way, step - 2, q)
+        return pltpu.make_async_remote_copy(
+            src_ref=block,
+            dst_ref=block,
+            send_sem=l_send.at[sem],
+            recv_sem=l_recv.at[sem],
+            device_id=neighbour(0, by),
+            device_id_type=MESH,
+        )
+
+    def rows_of(p):
+        return pl.ds(pl.multiple_of(step_x(p) * 128, 128), 128)
+
+    def product(p, nears, columns):
+        total = None
+        for near in nears:
+            chunk = along(z, near)
+            for part in (0, 1):
+                term = jnp.dot(
+                    yg[chunk, part, rows_of(p), :], xg[chunk, part, :, columns], preferred_element_type=jnp.float32
+                )
+                total = term if total is None else total + term
+        return total
+
+    sent = list(deals)
+    have = [set(), set()]
+
+    def take(kind, way, step, p):
+        if step == 0:
+            if p in have[kind]:
+                return
+            have[kind].add(p)
+            if p == 0:
+                own[kind].wait()
+                dealt(kind, 0, other).wait_recv()
+            else:
+                dealt(kind, p, 0).wait_recv()
+                dealt(kind, p, 1).wait_recv()
+        else:
+            arrived(kind, way, step, p).wait_recv()
+
+    taken = set()
+
+    def turn(kind, way, i):
+        step, p = ORDERS[kind][way][i]
+        take(kind, way, step, p)
+        taken.add((kind, way, step, p))
+        if kind == 0 and i >= 12:
+            return
+        copy = forward(kind, way, step, p)
+        copy.start()
+        sent.append(copy)
+
+    for i in range(14):
+        for kind in (0, 1):
+            for way in (0, 1):
+                turn(kind, way, i)
+    for q in range(4):
+        for i in (12, 13):
+            for way in (0, 1):
+                copy = last(way, *ORDERS[0][way][i], q)
+                copy.start()
+                sent.append(copy)
+    lasts = [(way, *ORDERS[0][way][i]) for i in (12, 13) for way in (0, 1)]
+    late = {(way, step + 1, p) for way, step, p in lasts}
+    for kind in (0, 1):
+        for way in (0, 1):
+            for step, p in ORDERS[kind][way]:
+                key = (kind, way, step + 1, p)
+                if key in taken or (kind == 0 and key[1:] in late) or (kind == 1 and p < 2):
+                    continue
+                arrived(*key).wait_recv()
+                taken.add(key)
+
+    def rest(p):
+        for way in (0, 1):
+            for step, p_of in ORDERS[1][way]:
+                key = (1, way, step + 1, p_of)
+                if p_of == p and key not in taken:
+                    arrived(*key).wait_recv()
+                    taken.add(key)
+
+    def hand(p, q):
+        return pltpu.make_async_remote_copy(
+            src_ref=tile.at[p, quarter(q)],
+            dst_ref=out_ref.at[x, quarter(q)],
+            send_sem=c_send.at[p, q],
+            recv_sem=c_recv.at[BACK[p], q],
             device_id=at(row, z, step_x(p), layer),
             device_id_type=MESH,
         )
 
-    hands = []
-    for p in (3, 1, 2, 0):
-        x_to = step_x(p)
-        rows = acc[pl.ds(pl.multiple_of(x_to * 128, 128), 128), :]
-        block = rows.T.astype(jnp.bfloat16)
+    def handed(p, q):
+        block = out_ref.at[step_x(p), quarter(q)]
+        return pltpu.make_async_remote_copy(
+            src_ref=block,
+            dst_ref=block,
+            send_sem=c_send.at[p, q],
+            recv_sem=c_recv.at[p, q],
+            device_id=at(row, z, step_x(p), layer),
+            device_id_type=MESH,
+        )
+
+    def early(p):
+        acc[p] = product(p, (0, 1, -1, 2, -2), slice(None))
+
+    def finish(p, q):
+        block = (acc[p, :, quarter(q)] + product(p, (3, -3, 4), quarter(q))).T.astype(jnp.bfloat16)
         if p == 0:
-            out_ref[x] = block
+            out_ref[x, quarter(q)] = block
         else:
-            tile[p] = block
-            copy = hand(p)
+            tile[p, quarter(q)] = block
+            copy = hand(p, q)
             copy.start()
-            hands.append(copy)
-    for copy in deals + forwards + hands:
+            sent.append(copy)
+
+    early(3)
+    early(2)
+    for q in range(4):
+        for key in lasts:
+            last_arrived(*key, q).wait_recv()
+        finish(3, q)
+        finish(2, q)
+        if q == 0:
+            rest(1)
+            early(1)
+        finish(1, q)
+    rest(0)
+    early(0)
+    for q in range(4):
+        finish(0, q)
+    for copy in sent:
         copy.wait_send()
     for p in (1, 2, 3):
-        handed(p).wait_recv()
+        for q in range(4):
+            handed(p, q).wait_recv()
 
 
 def on_device(anomaly_x, anomaly_y):
     dma = pltpu.SemaphoreType.DMA
     return pl.pallas_call(
         kernel,
-        out_shape=jax.ShapeDtypeStruct((4, 512, 128), jnp.bfloat16),
+        out_shape=pltpu.VMEM((4, 512, 128), jnp.bfloat16),
         in_specs=[pl.BlockSpec(memory_space=pl.ANY)] * 2,
         out_specs=pl.BlockSpec(memory_space=pltpu.VMEM),
         scratch_shapes=[
@@ -213,7 +301,7 @@
             pltpu.VMEM((8, 128, 256), jnp.bfloat16),
             pltpu.VMEM((RING, 2, 256, 512), jnp.bfloat16),
             pltpu.VMEM((RING, 2, 512, 256), jnp.bfloat16),
-            pltpu.VMEM((512, 512), jnp.float32),
+            pltpu.VMEM((LINE, 128, 512), jnp.float32),
             pltpu.VMEM((LINE, 512, 128), jnp.bfloat16),
             dma((2,)),
             dma((2,)),
@@ -221,8 +309,10 @@
             dma((2, LINE, 2)),
             dma((2, 2, 4, LINE)),
             dma((2, RING, LINE)),
-            dma((LINE,)),
-            dma((LINE,)),
+            dma((2, 2, 4)),
+            dma((2, 2, 4)),
+            dma((LINE, 4)),
+            dma((LINE, 4)),
         ],
         compiler_params=pltpu.CompilerParams(collective_id=0, has_side_effects=True),
     )(jnp.transpose(anomaly_x, (0, 2, 1)), anomaly_y)

time: 72.7 us -> 66.9 us (0.920)
  Pallas kernels: 70.7 us -> 66 us
  local copies, waits for them, and re-layouts: 1.87 us -> 0.8 us
    pallas_call x1, Pallas kernels: 70.7 us -> 66 us  [on_device(): pl.pallas_call(kernel, out_shape=pltpu.VMEM((4, 512, 128), jnp.bfloat16),...]
    unnamed x1, local copies, waits for them, and re-layouts: 1.87 us -> 0.8 us
where the time goes in v2:
time: 66.9 us; the launch traced here: 66.8 us
  Pallas kernels  66 us (99%)
  local copies, waits for them, and re-layouts  0.8 us (1%)
    pallas_call x1, Pallas kernels, on_device(): pl.pallas_call(kernel, out_shape=pltpu.VMEM((4, 512, 128), jnp.bfloat16),...  66 us

profile of v2, /device:TPU:1, one launch (start us, length us, event | category | flops | bytes accessed | tf_op | source)
XLA Modules:
  0.0 66.8 jit_solution(10379036759505451765)
XLA Ops:
  0.0 66.0 %shard_map.28 = bf16[4,512,128]{2,1,0:T(8,128)(2,1)S(1)} custom-call(bf16[8,64,512]{2,1,0:T(8,128)(2,1)} %bitcast.1, bf16[8,128,256]{2,1,0:T(8,128)(2,1)} %y_hbm.1), custom_call_target="tpu_custom_call" | custom-call | tf_op jit(solution)/shard_map/pallas_call | solution.py:294
  66.0 0.8 %copy.4 = bf16[4,512,128]{2,1,0:T(8,128)(2,1)} copy(bf16[4,512,128]{2,1,0:T(8,128)(2,1)S(1)} %shard_map.28) | data formatting | bytes 1048576

commit v3 on v0

v3 whole, which is shorter than its diff:
```python
import jax
import jax.numpy as jnp
from jax import lax
from jax.experimental import pallas as pl
from jax.experimental.pallas import tpu as pltpu
from jax.sharding import PartitionSpec as P

MESH = pl.DeviceIdType.MESH
RING = 8
LINE = 4
OFFSETS = (0, 1, 3, 2)
BACK = (0, 2, 1, 3)
UNITS = {"a": ("a",), "b": ("b",), 0: ("a", "b"), 1: (1,), 2: (2,), 3: (3,), "A": ("a", "b", 3), "B": (1, 2)}
SLOT = {"a": 0, "b": 4, 0: 0, 1: 1, 2: 2, 3: 3, "A": 5, "B": 6}
TURNS = (
    (0, 0, 0, "a"), (0, 1, 0, "a"), (1, 0, 0, "a"), (1, 1, 0, "a"), (0, 0, 0, "b"), (0, 1, 0, "b"),
    (1, 0, 0, "b"), (1, 1, 0, "b"), (0, 0, 1, "a"), (0, 1, 1, "a"), (1, 0, 1, "a"), (1, 1, 1, "a"),
    (0, 0, 0, 1), (0, 1, 0, 1), (1, 0, 0, 2), (1, 1, 0, 2), (1, 0, 1, "b"), (0, 0, 0, 2),
    (0, 1, 0, 2), (1, 1, 0, 1), (1, 0, 0, 1), (0, 0, 1, "b"), (0, 1, 1, "b"), (1, 1, 1, 2),
    (1, 0, 1, 2), (0, 0, 0, 3), (0, 1, 0, 3), (0, 0, 1, "B"), (0, 1, 1, "B"), (1, 1, 0, 3),
    (1, 0, 0, 3), (1, 1, 1, 1), (1, 0, 2, 0), (1, 1, 1, "b"), (0, 0, 1, 3), (0, 1, 1, 3),
    (1, 1, 1, 3), (1, 0, 1, 3), (0, 0, 2, 0), (1, 0, 1, 1), (1, 1, 2, "B"), (0, 1, 2, "B"),
    (0, 0, 2, 3), (1, 0, 2, 3), (0, 1, 2, "A"), (0, 0, 2, "B"), (1, 1, 2, 3), (1, 0, 2, 2),
    (1, 1, 3, 2), (0, 1, 3, "B"), (1, 0, 3, 3), (0, 0, 3, "A"), (1, 1, 3, 1), (1, 0, 2, 1),
    (1, 1, 2, 0), (1, 0, 3, 0),)


def kernel(
    x_hbm, y_hbm, out_ref, x_in, y_in, xg, yg, acc, tile, in_sem, own_sem,
    a_send, a_recv, g_send, g_recv, l_send, l_recv, c_send, c_recv,
):
    row, col, layer = lax.axis_index("row"), lax.axis_index("col"), lax.axis_index("layer")
    z, x = col // LINE, lax.rem(col, LINE)
    other = 1 - layer
    mine = layer * LINE + x

    def at(row_to, z_to, x_to, layer_to):
        return {"row": row_to, "col": z_to * LINE + x_to, "layer": layer_to}

    def step_x(p):
        return lax.rem(x + OFFSETS[p], LINE)

    def along(pos, by):
        return lax.rem(pos + by + RING, RING)

    def send(src, dst, send_sem, recv_sem, device_id):
        return pltpu.make_async_remote_copy(
            src_ref=src, dst_ref=dst, send_sem=send_sem, recv_sem=recv_sem, device_id=device_id, device_id_type=MESH
        )

    pos = (z, row)
    inputs = (x_in, y_in)
    gathered = (xg, yg)

    def place(kind, chunk, part, x_from):
        return gathered[kind].at[chunk, part, x_from // 2, lax.rem(x_from, 2)]

    def pair(kind, chunk, which):
        parity = lax.rem(x + (0 if which == "A" else 1), 2)
        return gathered[kind].at[chunk, :, :, parity]

    def piece(kind, chunk, p):
        if p in ("A", "B"):
            return pair(kind, chunk, p)
        if p in ("a", "b"):
            return place(kind, chunk, layer if p == "a" else other, x)
        return place(kind, chunk, slice(None), step_x(p))

    def neighbour(kind, by):
        return at(row, along(z, by), x, layer) if kind == 0 else at(along(row, by), z, x, layer)

    loads = [
        pltpu.make_async_copy(x_hbm, x_in, in_sem.at[0]),
        pltpu.make_async_copy(y_hbm, y_in, in_sem.at[1]),
    ]
    own = [
        pltpu.make_async_copy(x_hbm.at[mine], place(0, z, layer, x), own_sem.at[0]),
        pltpu.make_async_copy(y_hbm.at[mine], place(1, row, layer, x), own_sem.at[1]),
    ]
    for copy in loads + own:
        copy.start()

    barrier = pltpu.get_barrier_semaphore()
    peers = [at(row, z, x, other)]
    peers += [at(row, z, step_x(p), to) for p in (1, 2, 3) for to in (0, 1)]
    peers += [neighbour(kind, by) for kind in (0, 1) for by in (1, -1)]
    for peer in peers:
        pl.semaphore_signal(barrier, inc=1, device_id=peer, device_id_type=MESH)
    pl.semaphore_wait(barrier, len(peers))
    for copy in loads:
        copy.wait()

    def deal(kind, p, to):
        x_to = step_x(p)
        return send(
            inputs[kind].at[to * LINE + x_to],
            place(kind, pos[kind], layer, x),
            a_send.at[kind, p, to],
            a_recv.at[kind, BACK[p], layer],
            at(row, z, x_to, to),
        )

    def dealt(kind, p, origin):
        block = place(kind, pos[kind], origin, step_x(p))
        return send(block, block, a_send.at[kind, p, origin], a_recv.at[kind, p, origin], at(row, z, x, other))

    deals = [deal(kind, 0, other) for kind in (0, 1)]
    for first, to in ((0, 0), (0, 1), (1, 0), (1, 1)):
        deals += [deal(first, 2, to), deal(1 - first, 1, 1 - to)]
    deals += [deal(kind, 3, to) for kind in (0, 1) for to in (0, 1)]
    for copy in deals:
        copy.start()

    def forward(kind, way, step, p):
        by = 1 if way == 0 else -1
        chunk = along(pos[kind], -by * step)
        block = piece(kind, chunk, p)
        return send(block, block, g_send.at[kind, way, step, SLOT[p]], g_recv.at[kind, chunk, SLOT[p]], neighbour(kind, by))

    def arrived(kind, way, step, p):
        by = 1 if way == 0 else -1
        chunk = along(pos[kind], -by * step)
        block = piece(kind, chunk, p)
        return send(block, block, g_send.at[kind, way, 0, 0], g_recv.at[kind, chunk, SLOT[p]], neighbour(kind, by))

    def quarter(q):
        return pl.ds(q * 128, 128)

    def last(way, q):
        by = 1 if way == 0 else -1
        block = pair(0, along(z, -by * 3), "AB"[way]).at[:, :, :, quarter(q)]
        return send(block, block, l_send.at[way, q], l_recv.at[way, q], neighbour(0, by))

    def last_arrived(way, q):
        block = pair(0, along(z, 4), "AB"[way]).at[:, :, :, quarter(q)]
        return send(block, block, l_send.at[way, q], l_recv.at[way, q], neighbour(0, 1))

    sent = list(deals)
    taken = set()

    def new(*key):
        first = key not in taken
        taken.add(key)
        return first

    def come(kind, way, step, p):
        if new(kind, way, step, p):
            arrived(kind, way, step, p).wait_recv()

    def take(kind, way, step, p):
        for unit in UNITS[p]:
            if step > 0:
                for k, w, s, block in TURNS:
                    if (k, w, s) == (kind, way, step - 1) and unit in UNITS[block]:
                        come(kind, way, step, block)
            elif not new(kind, unit):
                continue
            elif unit == "a":
                own[kind].wait()
            elif unit == "b":
                dealt(kind, 0, other).wait_recv()
            else:
                dealt(kind, unit, 0).wait_recv()
                dealt(kind, unit, 1).wait_recv()

    def go(copies):
        for copy in copies:
            copy.start()
            sent.append(copy)

    for kind, way, step, p in TURNS:
        take(kind, way, step, p)
        if kind == 0 and step == 3:
            go([last(way, q) for q in range(4)])
        else:
            go([forward(kind, way, step, p)])

    def rest(kind, units):
        for k, way, step, p in TURNS:
            if k == kind and (kind, step) != (0, 3) and any(unit in units for unit in UNITS[p]):
                come(kind, way, step + 1, p)

    def product(p, nears, columns):
        x_from, total = step_x(p), None
        for near in nears:
            chunk = along(z, near)
            for part in (0, 1):
                left = yg[chunk, part, x_from // 2, lax.rem(x_from, 2)]
                right = xg[chunk, part, :, :, :, columns]
                right = right.reshape(256, right.shape[-1])
                term = jnp.dot(left, right, preferred_element_type=jnp.float32)
                total = term if total is None else total + term
        return total

    def hand(p, q):
        return send(
            tile.at[p, quarter(q)],
            out_ref.at[x, quarter(q)],
            c_send.at[p, q],
            c_recv.at[BACK[p], q],
            at(row, z, step_x(p), layer),
        )

    def handed(p, q):
        block = out_ref.at[step_x(p), quarter(q)]
        return send(block, block, c_send.at[p, q], c_recv.at[p, q], at(row, z, step_x(p), layer))

    def early(p):
        acc[p] = product(p, (0, 1, -1, 2, -2, 3, -3), slice(None))

    def finish(p, q):
        block = (acc[p, :, quarter(q)] + product(p, (4,), quarter(q))).T.astype(jnp.bfloat16)
        if p == 0:
            out_ref[x, quarter(q)] = block
        else:
            tile[p, quarter(q)] = block
            go([hand(p, q)])

    rest(0, ("a", "b", 1, 2, 3))
    rest(1, (2, 3))
    early(3)
    early(2)
    for q in range(4):
        for way in (0, 1):
            last_arrived(way, q).wait_recv()
        finish(3, q)
        finish(2, q)
        if q == 1:
            rest(1, (1,))
            early(1)
            finish(1, 0)
        if q >= 1:
            finish(1, q)
    rest(1, ("a", "b"))
    early(0)
    for q in range(4):
        finish(0, q)
    for copy in sent:
        copy.wait_send()
    for p in (1, 2, 3):
        for q in range(4):
            handed(p, q).wait_recv()


def on_device(anomaly_x, anomaly_y):
    dma = pltpu.SemaphoreType.DMA
    return pl.pallas_call(
        kernel,
        out_shape=pltpu.VMEM((4, 512, 128), jnp.bfloat16),
        in_specs=[pl.BlockSpec(memory_space=pl.ANY)] * 2,
        out_specs=pl.BlockSpec(memory_space=pltpu.VMEM),
        scratch_shapes=[
            pltpu.VMEM((8, 64, 512), jnp.bfloat16),
            pltpu.VMEM((8, 128, 256), jnp.bfloat16),
            pltpu.VMEM((RING, 2, 2, 2, 64, 512), jnp.bfloat16),
            pltpu.VMEM((RING, 2, 2, 2, 128, 256), jnp.bfloat16),
            pltpu.VMEM((LINE, 128, 512), jnp.float32),
            pltpu.VMEM((LINE, 512, 128), jnp.bfloat16),
            dma((2,)),
            dma((2,)),
            dma((2, LINE, 2)),
            dma((2, LINE, 2)),
            dma((2, 2, 4, 7)),
            dma((2, RING, 7)),
            dma((2, 4)),
            dma((2, 4)),
            dma((LINE, 4)),
            dma((LINE, 4)),
        ],
        compiler_params=pltpu.CompilerParams(collective_id=0, has_side_effects=True),
    )(jnp.transpose(anomaly_x, (0, 2, 1)), anomaly_y)


def solution(mesh):
    placed = (P(None, "row", ("layer", "col")), P(None, "col", ("layer", "row")))
    return jax.shard_map(
        on_device, mesh=mesh, in_specs=placed, out_specs=P("layer", "row", "col"), check_vma=False
    )
```

time: 186 us -> 64 us (0.34)
  blocking collectives: 107 us -> 0 us
  Pallas kernels: 0 us -> 63.1 us
  waiting for transfers between devices: 49.8 us -> 0 us
  between operations: 13.4 us -> 0.01 us
  matrix products: 9.82 us -> 0 us
  local copies, waits for them, and re-layouts: 4.08 us -> 0.8 us
    all_to_all x2 -> x0, blocking collectives: 107 us -> none  [the longest x1 101 us: copy_for_each(): return lax.all_to_all(copies, axis, split_axis=0, concat_axis=0, tiled=True)]
    pallas_call x0 -> x1, Pallas kernels: none -> 63.1 us  [on_device(): pl.pallas_call(kernel, out_shape=pltpu.VMEM((4, 512, 128), jnp.bfloat16),...]
    all_gather x1 -> x0, waiting for transfers between devices: 49.1 us -> none  [on_device(): panel_x = lax.all_gather(anomaly_x, 'col', axis=2, tiled=True)]
    dot_general x1 -> x0, matrix products: 9.82 us -> none  [on_device(): jnp.einsum('bik,bjk->bij', panel_x, collect(anomaly_y, 'row', 2), preferr...]
    reshape x1 -> x0, local copies, waits for them, and re-layouts: 2.52 us -> none  [laid_out(): return jnp.moveaxis(tiles, 0, dim).reshape(lengths)]
  transfers between devices with their start and end apart: 1 -> 0, of which waited for: 1 -> 0; matrix products, arithmetic and copies ran while one was open for 2% -> 0% of each run, Pallas kernels for 0% -> 0%
where the time goes in v3:
time: 64 us; the launch traced here: 63.9 us
  Pallas kernels  63.1 us (99%)
  local copies, waits for them, and re-layouts  0.8 us (1%)
    pallas_call x1, Pallas kernels, on_device(): pl.pallas_call(kernel, out_shape=pltpu.VMEM((4, 512, 128), jnp.bfloat16),...  63.1 us

profile of v3, /device:TPU:1, one launch (start us, length us, event | category | flops | bytes accessed | tf_op | source)
XLA Modules:
  0.0 63.9 jit_solution(4499396907098908587)
XLA Ops:
  0.0 63.1 %shard_map.28 = bf16[4,512,128]{2,1,0:T(8,128)(2,1)S(1)} custom-call(bf16[8,64,512]{2,1,0:T(8,128)(2,1)} %bitcast.1, bf16[8,128,256]{2,1,0:T(8,128)(2,1)} %y_hbm.1), custom_call_target="tpu_custom_call" | custom-call | tf_op jit(solution)/shard_map/pallas_call | solution.py:247
  63.1 0.8 %copy.4 = bf16[4,512,128]{2,1,0:T(8,128)(2,1)} copy(bf16[4,512,128]{2,1,0:T(8,128)(2,1)S(1)} %shard_map.28) | data formatting | bytes 1048576

commit v4 on v3

--- a/solution.py
+++ b/solution.py
@@ -11,23 +11,24 @@
 OFFSETS = (0, 1, 3, 2)
 BACK = (0, 2, 1, 3)
 UNITS = {"a": ("a",), "b": ("b",), 0: ("a", "b"), 1: (1,), 2: (2,), 3: (3,), "A": ("a", "b", 3), "B": (1, 2)}
-SLOT = {"a": 0, "b": 4, 0: 0, 1: 1, 2: 2, 3: 3, "A": 5, "B": 6}
 TURNS = (
     (0, 0, 0, "a"), (0, 1, 0, "a"), (1, 0, 0, "a"), (1, 1, 0, "a"), (0, 0, 0, "b"), (0, 1, 0, "b"),
-    (1, 0, 0, "b"), (1, 1, 0, "b"), (0, 0, 1, "a"), (0, 1, 1, "a"), (1, 0, 1, "a"), (1, 1, 1, "a"),
-    (0, 0, 0, 1), (0, 1, 0, 1), (1, 0, 0, 2), (1, 1, 0, 2), (1, 0, 1, "b"), (0, 0, 0, 2),
-    (0, 1, 0, 2), (1, 1, 0, 1), (1, 0, 0, 1), (0, 0, 1, "b"), (0, 1, 1, "b"), (1, 1, 1, 2),
-    (1, 0, 1, 2), (0, 0, 0, 3), (0, 1, 0, 3), (0, 0, 1, "B"), (0, 1, 1, "B"), (1, 1, 0, 3),
-    (1, 0, 0, 3), (1, 1, 1, 1), (1, 0, 2, 0), (1, 1, 1, "b"), (0, 0, 1, 3), (0, 1, 1, 3),
-    (1, 1, 1, 3), (1, 0, 1, 3), (0, 0, 2, 0), (1, 0, 1, 1), (1, 1, 2, "B"), (0, 1, 2, "B"),
-    (0, 0, 2, 3), (1, 0, 2, 3), (0, 1, 2, "A"), (0, 0, 2, "B"), (1, 1, 2, 3), (1, 0, 2, 2),
-    (1, 1, 3, 2), (0, 1, 3, "B"), (1, 0, 3, 3), (0, 0, 3, "A"), (1, 1, 3, 1), (1, 0, 2, 1),
-    (1, 1, 2, 0), (1, 0, 3, 0),)
+    (1, 0, 0, "b"), (1, 1, 0, "b"), (0, 0, 1, "a"), (0, 1, 1, "a"), (1, 1, 1, "a"), (1, 0, 0, 2),
+    (0, 0, 0, 1), (0, 1, 0, 1), (1, 0, 1, "a"), (1, 1, 0, 2), (0, 0, 0, 2), (0, 1, 0, 2),
+    (1, 0, 0, 1), (1, 1, 0, 1), (0, 0, 1, "b"), (0, 1, 1, "b"), (1, 1, 1, "b"), (1, 0, 1, "b"),
+    (1, 0, 1, 2), (0, 0, 1, 1), (0, 1, 1, 1), (1, 1, 1, 2), (1, 1, 1, 1), (0, 0, 0, 3),
+    (0, 1, 0, 3), (0, 0, 1, 2), (0, 1, 1, 2), (1, 0, 0, 3), (1, 0, 1, 1), (1, 1, 0, 3),
+    (0, 1, 2, 1), (1, 1, 2, 2), (0, 0, 1, 3), (0, 0, 2, 0), (0, 1, 1, 3), (1, 0, 1, 3),
+    (1, 0, 2, 0), (1, 1, 1, 3), (0, 1, 2, 2), (1, 1, 2, 1), (0, 1, 2, 0), (1, 1, 3, 2),
+    (0, 0, 2, 3), (0, 0, 2, "B"), (1, 0, 2, 3), (1, 0, 2, 2), (0, 1, 2, 3), (1, 1, 2, 3),
+    (0, 1, 3, "B"), (1, 1, 3, 1), (0, 0, 3, "A"), (1, 0, 3, 3), (1, 0, 2, 1), (1, 1, 2, 0),
+    (1, 0, 3, 0),)
+SLOT = {turn: i for i, turn in enumerate(t for t in TURNS if (t[0], t[2]) != (0, 3))}
 
 
 def kernel(
     x_hbm, y_hbm, out_ref, x_in, y_in, xg, yg, acc, tile, in_sem, own_sem,
-    a_send, a_recv, g_send, g_recv, l_send, l_recv, c_send, c_recv,
+    a_send, a_recv, g_send, g_recv, l_recv, c_send, c_recv,
 ):
     row, col, layer = lax.axis_index("row"), lax.axis_index("col"), lax.axis_index("layer")
     z, x = col // LINE, lax.rem(col, LINE)
@@ -95,14 +96,15 @@
         return send(
             inputs[kind].at[to * LINE + x_to],
             place(kind, pos[kind], layer, x),
-            a_send.at[kind, p, to],
-            a_recv.at[kind, BACK[p], layer],
+            a_send.at[kind],
+            a_recv.at[kind, BACK[p]],
             at(row, z, x_to, to),
         )
 
-    def dealt(kind, p, origin):
-        block = place(kind, pos[kind], origin, step_x(p))
-        return send(block, block, a_send.at[kind, p, origin], a_recv.at[kind, p, origin], at(row, z, x, other))
+    def dealt(kind, p):
+        part = other if p == 0 else slice(None)
+        block = place(kind, pos[kind], part, step_x(p))
+        return send(block, block, a_send.at[kind], a_recv.at[kind, p], at(row, z, x, other))
 
     deals = [deal(kind, 0, other) for kind in (0, 1)]
     for first, to in ((0, 0), (0, 1), (1, 0), (1, 1)):
@@ -115,13 +117,13 @@
         by = 1 if way == 0 else -1
         chunk = along(pos[kind], -by * step)
         block = piece(kind, chunk, p)
-        return send(block, block, g_send.at[kind, way, step, SLOT[p]], g_recv.at[kind, chunk, SLOT[p]], neighbour(kind, by))
+        return send(block, block, g_send.at[kind], g_recv.at[SLOT[kind, way, step, p]], neighbour(kind, by))
 
     def arrived(kind, way, step, p):
         by = 1 if way == 0 else -1
         chunk = along(pos[kind], -by * step)
         block = piece(kind, chunk, p)
-        return send(block, block, g_send.at[kind, way, 0, 0], g_recv.at[kind, chunk, SLOT[p]], neighbour(kind, by))
+        return send(block, block, g_send.at[kind], g_recv.at[SLOT[kind, way, step - 1, p]], neighbour(kind, by))
 
     def quarter(q):
         return pl.ds(q * 128, 128)
@@ -129,13 +131,12 @@
     def last(way, q):
         by = 1 if way == 0 else -1
         block = pair(0, along(z, -by * 3), "AB"[way]).at[:, :, :, quarter(q)]
-        return send(block, block, l_send.at[way, q], l_recv.at[way, q], neighbour(0, by))
-
-    def last_arrived(way, q):
-        block = pair(0, along(z, 4), "AB"[way]).at[:, :, :, quarter(q)]
-        return send(block, block, l_send.at[way, q], l_recv.at[way, q], neighbour(0, 1))
-
-    sent = list(deals)
+        return send(block, block, g_send.at[0], l_recv.at[q], neighbour(0, by))
+
+    def last_arrived(q):
+        block = xg.at[along(z, 4), :, :, :, :, quarter(q)]
+        return send(block, block, g_send.at[0], l_recv.at[q], neighbour(0, 1))
+
     taken = set()
 
     def new(*key):
@@ -158,15 +159,13 @@
             elif unit == "a":
                 own[kind].wait()
             elif unit == "b":
-                dealt(kind, 0, other).wait_recv()
+                dealt(kind, 0).wait_recv()
             else:
-                dealt(kind, unit, 0).wait_recv()
-                dealt(kind, unit, 1).wait_recv()
+                dealt(kind, unit).wait_recv()
 
     def go(copies):
         for copy in copies:
             copy.start()
-            sent.append(copy)
 
     for kind, way, step, p in TURNS:
         take(kind, way, step, p)
@@ -196,14 +195,10 @@
         return send(
             tile.at[p, quarter(q)],
             out_ref.at[x, quarter(q)],
-            c_send.at[p, q],
-            c_recv.at[BACK[p], q],
+            c_send,
+            c_recv,
             at(row, z, step_x(p), layer),
         )
-
-    def handed(p, q):
-        block = out_ref.at[step_x(p), quarter(q)]
-        return send(block, block, c_send.at[p, q], c_recv.at[p, q], at(row, z, step_x(p), layer))
 
     def early(p):
         acc[p] = product(p, (0, 1, -1, 2, -2, 3, -3), slice(None))
@@ -221,8 +216,7 @@
     early(3)
     early(2)
     for q in range(4):
-        for way in (0, 1):
-            last_arrived(way, q).wait_recv()
+        last_arrived(q).wait_recv()
         finish(3, q)
         finish(2, q)
         if q == 1:
@@ -235,11 +229,14 @@
     early(0)
     for q in range(4):
         finish(0, q)
-    for copy in sent:
-        copy.wait_send()
-    for p in (1, 2, 3):
-        for q in range(4):
-            handed(p, q).wait_recv()
+    for kind in (0, 1):
+        batches, chunks = inputs[kind].at[: RING - 1], gathered[kind].at[: RING - 1]
+        send(batches, batches, a_send.at[kind], a_recv.at[kind, 0], neighbour(kind, 1)).wait_send()
+        send(chunks, chunks, g_send.at[kind], g_recv.at[0], neighbour(kind, 1)).wait_send()
+    tiles = tile.at[1:]
+    handed = send(tiles, tiles, c_send, c_recv, at(row, z, step_x(1), layer))
+    handed.wait_send()
+    handed.wait_recv()
 
 
 def on_device(anomaly_x, anomaly_y):
@@ -258,14 +255,13 @@
             pltpu.VMEM((LINE, 512, 128), jnp.bfloat16),
             dma((2,)),
             dma((2,)),
-            dma((2, LINE, 2)),
-            dma((2, LINE, 2)),
-            dma((2, 2, 4, 7)),
-            dma((2, RING, 7)),
-            dma((2, 4)),
-            dma((2, 4)),
-            dma((LINE, 4)),
-            dma((LINE, 4)),
+            dma((2,)),
+            dma((2, LINE)),
+            dma((2,)),
+            dma((len(SLOT),)),
+            dma((4,)),
+            dma,
+            dma,
         ],
         compiler_params=pltpu.CompilerParams(collective_id=0, has_side_effects=True),
     )(jnp.transpose(anomaly_x, (0, 2, 1)), anomaly_y)

time: 64 us -> 62.9 us (0.983)
  Pallas kernels: 63.1 us -> 61.7 us
    pallas_call x1, Pallas kernels: 63.1 us -> 61.7 us  [on_device(): pl.pallas_call(kernel, out_shape=pltpu.VMEM((4, 512, 128), jnp.bfloat16),...]
where the time goes in v4:
time: 62.9 us; the launch traced here: 62.5 us
  Pallas kernels  61.7 us (98%)
  local copies, waits for them, and re-layouts  0.8 us (1%)
    pallas_call x1, Pallas kernels, on_device(): pl.pallas_call(kernel, out_shape=pltpu.VMEM((4, 512, 128), jnp.bfloat16),...  61.7 us

profile of v4, /device:TPU:1, one launch (start us, length us, event | category | flops | bytes accessed | tf_op | source)
XLA Modules:
  0.0 62.5 jit_solution(18123530342729137494)
XLA Ops:
  0.0 61.7 %shard_map.28 = bf16[4,512,128]{2,1,0:T(8,128)(2,1)S(1)} custom-call(bf16[8,64,512]{2,1,0:T(8,128)(2,1)} %bitcast.1, bf16[8,128,256]{2,1,0:T(8,128)(2,1)} %y_hbm.1), custom_call_target="tpu_custom_call" | custom-call | tf_op jit(solution)/shard_map/pallas_call | solution.py:244
  61.7 0.8 %copy.4 = bf16[4,512,128]{2,1,0:T(8,128)(2,1)} copy(bf16[4,512,128]{2,1,0:T(8,128)(2,1)S(1)} %shard_map.28) | data formatting | bytes 1048576

commit v5 on v4

--- a/solution.py
+++ b/solution.py
@@ -219,12 +219,10 @@
         last_arrived(q).wait_recv()
         finish(3, q)
         finish(2, q)
-        if q == 1:
+        if q == 0:
             rest(1, (1,))
             early(1)
-            finish(1, 0)
-        if q >= 1:
-            finish(1, q)
+        finish(1, q)
     rest(1, ("a", "b"))
     early(0)
     for q in range(4):

time: 62.9 us -> 62.5 us (level)
  no operation moved by 1% of the time
where the time goes in v5:
time: 62.5 us; the launch traced here: 62.1 us
  Pallas kernels  61.3 us (98%)
  local copies, waits for them, and re-layouts  0.8 us (1%)
    pallas_call x1, Pallas kernels, on_device(): pl.pallas_call(kernel, out_shape=pltpu.VMEM((4, 512, 128), jnp.bfloat16),...  61.3 us

profile of v5, /device:TPU:1, one launch (start us, length us, event | category | flops | bytes accessed | tf_op | source)
XLA Modules:
  0.0 62.1 jit_solution(5960226765553142362)
XLA Ops:
  0.0 61.3 %shard_map.28 = bf16[4,512,128]{2,1,0:T(8,128)(2,1)S(1)} custom-call(bf16[8,64,512]{2,1,0:T(8,128)(2,1)} %bitcast.1, bf16[8,128,256]{2,1,0:T(8,128)(2,1)} %y_hbm.1), custom_call_target="tpu_custom_call" | custom-call | tf_op jit(solution)/shard_map/pallas_call | solution.py:242
  61.3 0.8 %copy.4 = bf16[4,512,128]{2,1,0:T(8,128)(2,1)} copy(bf16[4,512,128]{2,1,0:T(8,128)(2,1)S(1)} %shard_map.28) | data formatting | bytes 1048576

commit v6 on v5

--- a/solution.py
+++ b/solution.py
@@ -192,9 +192,10 @@
         return total
 
     def hand(p, q):
+        rows = pl.ds(0, 256) if (p, q) == (1, 1) else quarter(q)
         return send(
-            tile.at[p, quarter(q)],
-            out_ref.at[x, quarter(q)],
+            tile.at[p, rows],
+            out_ref.at[x, rows],
             c_send,
             c_recv,
             at(row, z, step_x(p), layer),
@@ -209,7 +210,8 @@
             out_ref[x, quarter(q)] = block
         else:
             tile[p, quarter(q)] = block
-            go([hand(p, q)])
+            if (p, q) != (1, 0):
+                go([hand(p, q)])
 
     rest(0, ("a", "b", 1, 2, 3))
     rest(1, (2, 3))

time: 62.5 us -> 62.6 us (level)
  no operation moved by 1% of the time
where the time goes in v6:
time: 62.6 us; the launch traced here: 62.1 us
  Pallas kernels  61.3 us (98%)
  local copies, waits for them, and re-layouts  0.8 us (1%)
    pallas_call x1, Pallas kernels, on_device(): pl.pallas_call(kernel, out_shape=pltpu.VMEM((4, 512, 128), jnp.bfloat16),...  61.3 us

profile of v6, /device:TPU:1, one launch (start us, length us, event | category | flops | bytes accessed | tf_op | source)
XLA Modules:
  0.0 62.1 jit_solution(13983644356090721463)
XLA Ops:
  0.0 61.3 %shard_map.28 = bf16[4,512,128]{2,1,0:T(8,128)(2,1)S(1)} custom-call(bf16[8,64,512]{2,1,0:T(8,128)(2,1)} %bitcast.1, bf16[8,128,256]{2,1,0:T(8,128)(2,1)} %y_hbm.1), custom_call_target="tpu_custom_call" | custom-call | tf_op jit(solution)/shard_map/pallas_call | solution.py:244
  61.3 0.8 %copy.4 = bf16[4,512,128]{2,1,0:T(8,128)(2,1)} copy(bf16[4,512,128]{2,1,0:T(8,128)(2,1)S(1)} %shard_map.28) | data formatting | bytes 1048576
